TPU v7x, 32 devices: a whole 2x2x4 slice. The times are simulated.
32 devices in a mesh: groups: 2 (over x), seq: 16 (over z, y, core).
Axes of the slice: x: 2, y: 2, z: 4, core: 2. Of those that a mesh axis runs over, the one named last changes fastest.
Arguments:
- candidates: bfloat16 [32, 256, 256], P('groups', 'seq'), parts along dimension 0, may hold values from -110 to 110
- codes: int32 [32, 2048, 256], P('groups', 'seq'), parts along dimension 0, may hold values from -2147483648 to 2147483647
- scale_index: int32 [32, 8192], P('groups', 'seq'), parts along dimension 0, may hold values from 0 to 255
- lengths: int32 [32], P('groups'), parts along dimension 0, may hold values from 128 to 8192, as said below
- scale_table: float32 [256], replicated, may hold values from 0.004 to 0.04
- query_weight: bfloat16 [256, 256], replicated, may hold values from -0.375 to 0.375
- key_weight: bfloat16 [256, 256], replicated, may hold values from -0.375 to 0.375
- value_weight: bfloat16 [256, 256], replicated, may hold values from -0.375 to 0.375
- out_weight: bfloat16 [256, 256], replicated, may hold values from -0.375 to 0.375
- norm_gain: float32 [256], replicated, may hold values from 0.1 to 1.9
- hidden_weight: bfloat16 [256, 512], replicated, may hold values from -0.375 to 0.375
- hidden_bias: float32 [512], replicated, may hold values from -4 to 4
- score_weight: bfloat16 [512], replicated, may hold values from -0.25 to 0.25
Outputs:
- interest: bfloat16 [32, 256, 256], P('groups', 'seq'), parts along dimension 0
- logits: float32 [32, 256], P('groups', 'seq'), parts along dimension 0
There are 2 independent parts, one for each index of `groups`. A program takes and returns all parts, laid end to end along the dimension named above; an argument that names none is the same for every part. Nothing has to cross between parts.
Inputs may be any that keep to these rules, and one draw needn't show every extreme that they name: `lengths`: each user's history length is a multiple of 128; in every draw some user's length is 8192.
All inputs are finite; a program needn't handle non-finite values.
Results may differ from a plain program's by a relative error of at most 0.02.
The roundings to bfloat16 on the way count: a program that leaves them out, or rounds other values in their place, can miss the bound.
Values may be sent and summed in bfloat16 or wider, within the bound.
A program may use at most 128 MiB of HBM per device.

v0:
```python
import math
import jax
import jax.numpy as jnp
from jax import lax
from jax.sharding import PartitionSpec as P

HEADS = 4
NEG_FILL = -1e30


def unpack_codes(words):
    byte_rows = [jnp.right_shift(jnp.left_shift(words, 24 - 8 * k), 24) for k in range(4)]
    stacked = jnp.stack(byte_rows, axis=1)
    return stacked.reshape(words.shape[0] * 4, words.shape[1])


def score_block(query_rows, key_rows, live_row):
    cand_rows, model_width = query_rows.shape
    head_size = model_width // HEADS
    split_query = query_rows.reshape(cand_rows, HEADS, head_size)
    split_keys = key_rows.reshape(key_rows.shape[0], HEADS, head_size)
    scores = jnp.einsum("chd,khd->hck", split_query, split_keys, preferred_element_type=jnp.float32)
    scores = scores * (1.0 / math.sqrt(head_size))
    return jnp.where(live_row[None, None, :], scores, NEG_FILL)


def exp_weights(scores, live_row, peak_rows):
    return jnp.where(live_row[None, None, :], jnp.exp(scores - peak_rows[:, :, None]), 0.0)


def weighted_rows(weights, value_rows):
    head_count, cand_rows, key_count = weights.shape
    split_values = value_rows.reshape(key_count, head_count, -1)
    blended = jnp.einsum(
        "hck,khd->chd",
        weights.astype(jnp.bfloat16),
        split_values,
        preferred_element_type=jnp.float32,
    )
    return blended.reshape(cand_rows, -1)


def local_partials(user_item):
    query_rows, key_rows, value_rows, live_row = user_item
    scores = score_block(query_rows, key_rows, live_row)
    peak_rows = jnp.max(scores, axis=2)
    weights = exp_weights(scores, live_row, peak_rows)
    return (weighted_rows(weights, value_rows), jnp.sum(weights, axis=2), peak_rows)


def on_device(
    candidates,
    codes,
    scale_index,
    lengths,
    scale_table,
    query_weight,
    key_weight,
    value_weight,
    out_weight,
    norm_gain,
    hidden_weight,
    hidden_bias,
    score_weight,
):
    user_count, cand_local, model_width = candidates.shape
    hist_local = scale_index.shape[1]
    head_size = model_width // HEADS
    own_queries = jnp.einsum(
        "ucd,de->uce", candidates, query_weight, preferred_element_type=jnp.float32
    ).astype(jnp.bfloat16)
    queries = lax.all_gather(own_queries, "seq", axis=1, tiled=True)
    offset = lax.axis_index("seq") * hist_local
    places = offset + jnp.arange(hist_local, dtype=jnp.int32)
    live_mask = places[None, :] < lengths[:, None]
    levels = jnp.arange(scale_table.shape[0], dtype=jnp.int32)

    def project(user_item):
        word_rows, index_rows = user_item
        code_rows = unpack_codes(word_rows)
        row_scales = jnp.sum(
            jnp.where(index_rows[:, None] == levels[None, :], scale_table[None, :], 0.0), axis=1
        )
        history = (code_rows.astype(jnp.float32) * row_scales[:, None]).astype(jnp.bfloat16)
        key_rows = jnp.dot(history, key_weight, preferred_element_type=jnp.float32).astype(
            jnp.bfloat16
        )
        value_rows = jnp.dot(history, value_weight, preferred_element_type=jnp.float32).astype(
            jnp.bfloat16
        )
        return (key_rows, value_rows)

    all_keys, all_values = lax.map(project, (codes, scale_index))
    numerators, totals, peak_rows = lax.map(
        local_partials, (queries, all_keys, all_values, live_mask)
    )
    got_numerators = lax.all_to_all(
        numerators[None].astype(jnp.bfloat16), "seq", split_axis=2, concat_axis=0, tiled=True
    ).astype(jnp.float32)
    got_peaks, got_totals = (
        lax.all_to_all(peak_rows[None], "seq", split_axis=3, concat_axis=0, tiled=True),
        lax.all_to_all(totals[None], "seq", split_axis=3, concat_axis=0, tiled=True),
    )
    global_peaks = jnp.max(got_peaks, axis=0)
    factor = jnp.exp(got_peaks - global_peaks[None])
    totals = jnp.sum(factor * got_totals, axis=0)
    sources = got_numerators.shape[0]
    scaled = (
        got_numerators.reshape(sources, user_count, cand_local, HEADS, head_size)
        * jnp.transpose(factor, (0, 1, 3, 2))[..., None]
    )
    numerators = jnp.sum(scaled, axis=0).reshape(user_count, cand_local, model_width)
    split_numer = numerators.reshape(user_count, cand_local, HEADS, head_size)
    attended = (
        (split_numer / jnp.transpose(totals, (0, 2, 1))[..., None])
        .reshape(user_count, cand_local, model_width)
        .astype(jnp.bfloat16)
    )
    interest = jnp.einsum(
        "ucd,de->uce", attended, out_weight, preferred_element_type=jnp.float32
    ).astype(jnp.bfloat16)
    floats = interest.astype(jnp.float32)
    normed = (
        floats * lax.rsqrt(jnp.mean(floats * floats, axis=2, keepdims=True) + 1e-06) * norm_gain
    ).astype(jnp.bfloat16)
    hidden = jax.nn.silu(
        jnp.einsum("ucd,dh->uch", normed, hidden_weight, preferred_element_type=jnp.float32)
        + hidden_bias
    ).astype(jnp.bfloat16)
    logits = jnp.einsum("uch,h->uc", hidden, score_weight, preferred_element_type=jnp.float32)
    return (interest, logits)


def solution(mesh):
    placed = (
        P("groups", "seq", None),
        P("groups", "seq", None),
        P("groups", "seq"),
        P("groups"),
        P(),
        P(),
        P(),
        P(),
        P(),
        P(),
        P(),
        P(),
        P(),
    )
    return jax.shard_map(
        on_device,
        mesh=mesh,
        in_specs=placed,
        out_specs=(P("groups", "seq", None), P("groups", "seq")),
        check_vma=False,
    )
```

profile of v0, /device:TPU:13, one launch (start us, length us, event | category | flops | bytes accessed | tf_op | source)
XLA Modules:
  0.0 369.4 jit_solution(11931711030557221657)
XLA Ops:
  7.2 1.8 convolution_convert_fusion.3
  9.1 80.3 %while.28 = (s32[]{:T(128)}, bf16[16,512,256]{2,1,0:T(8,128)(2,1)}, bf16[16,512,256]{2,1,0:T(8,128)(2,1)}, s32[16,128,256]{2,1,0:T(8,128)}, s32[16,512]{1,0:T(8,...) while((s32[]{:T(128)}, bf16[16,512,256]{2,1,0:T(8,128)(2,1)}, ...), condition=%wide.region_2.3_spmd.clone, body=%wide.region_0.2_spmd.clone.sunk | while | flops 136183296 | bytes 5916857 | solution.py:93
  27.2 1.0 fusion.65
  37.2 1.0 fusion.65
  89.5 191.5 %while.27 = (s32[]{:T(128)}, bf16[16,256,256]{2,0,1:T(8,128)(2,1)}, f32[16,4,256]{2,1,0:T(4,128)S(1)}, f32[16,4,256]{2,1,0:T(4,128)S(1)}, bf16[16,512,256]{2,1,0...) while((s32[]{:T(128)}, bf16[16,256,256]{2,0,1:T(8,128)(2,1)}, ...), condition=%wide.region_6.7_spmd, body=%wide.region_3.6_spmd.sunk | while | flops 141031424 | bytes 10259069 | solution.py:94
  94.8 6.6 %dynamic_update_slice.29 = bf16[16,256,256]{2,0,1:T(8,128)(2,1)} dynamic-update-slice(bf16[16,256,256]{2,0,1:T(8,128)(2,1)} %get-tuple-element.385, bf16[1,256,256]{2,0,1:T(2,128)(2,1)S(1)} %copy.82, s32[]{:T(128)} %get-tuple-element.384, s32[]{:T(128)} %constant.40.clone.1..sunk, s32[]{:T(128)} %constant.40.clone.1..sunk) | dynamic-update-slice | bytes 262148 | tf_op jit(solution)/shard_map/while/body/jit(dynamic_update_index_in_dim)/dynamic_update_slice | solution.py:94
  106.8 6.6 %dynamic_update_slice.29 = bf16[16,256,256]{2,0,1:T(8,128)(2,1)} dynamic-update-slice(bf16[16,256,256]{2,0,1:T(8,128)(2,1)} %get-tuple-element.385, bf16[1,256,256]{2,0,1:T(2,128)(2,1)S(1)} %copy.82, s32[]{:T(128)} %get-tuple-element.384, s32[]{:T(128)} %constant.40.clone.1..sunk, s32[]{:T(128)} %constant.40.clone.1..sunk) | dynamic-update-slice | bytes 262148 | tf_op jit(solution)/shard_map/while/body/jit(dynamic_update_index_in_dim)/dynamic_update_slice | solution.py:94
  118.8 6.6 %dynamic_update_slice.29 = bf16[16,256,256]{2,0,1:T(8,128)(2,1)} dynamic-update-slice(bf16[16,256,256]{2,0,1:T(8,128)(2,1)} %get-tuple-element.385, bf16[1,256,256]{2,0,1:T(2,128)(2,1)S(1)} %copy.82, s32[]{:T(128)} %get-tuple-element.384, s32[]{:T(128)} %constant.40.clone.1..sunk, s32[]{:T(128)} %constant.40.clone.1..sunk) | dynamic-update-slice | bytes 262148 | tf_op jit(solution)/shard_map/while/body/jit(dynamic_update_index_in_dim)/dynamic_update_slice | solution.py:94
  130.8 6.6 %dynamic_update_slice.29 = bf16[16,256,256]{2,0,1:T(8,128)(2,1)} dynamic-update-slice(bf16[16,256,256]{2,0,1:T(8,128)(2,1)} %get-tuple-element.385, bf16[1,256,256]{2,0,1:T(2,128)(2,1)S(1)} %copy.82, s32[]{:T(128)} %get-tuple-element.384, s32[]{:T(128)} %constant.40.clone.1..sunk, s32[]{:T(128)} %constant.40.clone.1..sunk) | dynamic-update-slice | bytes 262148 | tf_op jit(solution)/shard_map/while/body/jit(dynamic_update_index_in_dim)/dynamic_update_slice | solution.py:94
  142.7 6.6 %dynamic_update_slice.29 = bf16[16,256,256]{2,0,1:T(8,128)(2,1)} dynamic-update-slice(bf16[16,256,256]{2,0,1:T(8,128)(2,1)} %get-tuple-element.385, bf16[1,256,256]{2,0,1:T(2,128)(2,1)S(1)} %copy.82, s32[]{:T(128)} %get-tuple-element.384, s32[]{:T(128)} %constant.40.clone.1..sunk, s32[]{:T(128)} %constant.40.clone.1..sunk) | dynamic-update-slice | bytes 262148 | tf_op jit(solution)/shard_map/while/body/jit(dynamic_update_index_in_dim)/dynamic_update_slice | solution.py:94
  154.7 6.6 %dynamic_update_slice.29 = bf16[16,256,256]{2,0,1:T(8,128)(2,1)} dynamic-update-slice(bf16[16,256,256]{2,0,1:T(8,128)(2,1)} %get-tuple-element.385, bf16[1,256,256]{2,0,1:T(2,128)(2,1)S(1)} %copy.82, s32[]{:T(128)} %get-tuple-element.384, s32[]{:T(128)} %constant.40.clone.1..sunk, s32[]{:T(128)} %constant.40.clone.1..sunk) | dynamic-update-slice | bytes 262148 | tf_op jit(solution)/shard_map/while/body/jit(dynamic_update_index_in_dim)/dynamic_update_slice | solution.py:94
  166.7 6.6 %dynamic_update_slice.29 = bf16[16,256,256]{2,0,1:T(8,128)(2,1)} dynamic-update-slice(bf16[16,256,256]{2,0,1:T(8,128)(2,1)} %get-tuple-element.385, bf16[1,256,256]{2,0,1:T(2,128)(2,1)S(1)} %copy.82, s32[]{:T(128)} %get-tuple-element.384, s32[]{:T(128)} %constant.40.clone.1..sunk, s32[]{:T(128)} %constant.40.clone.1..sunk) | dynamic-update-slice | bytes 262148 | tf_op jit(solution)/shard_map/while/body/jit(dynamic_update_index_in_dim)/dynamic_update_slice | solution.py:94
  178.7 6.6 %dynamic_update_slice.29 = bf16[16,256,256]{2,0,1:T(8,128)(2,1)} dynamic-update-slice(bf16[16,256,256]{2,0,1:T(8,128)(2,1)} %get-tuple-element.385, bf16[1,256,256]{2,0,1:T(2,128)(2,1)S(1)} %copy.82, s32[]{:T(128)} %get-tuple-element.384, s32[]{:T(128)} %constant.40.clone.1..sunk, s32[]{:T(128)} %constant.40.clone.1..sunk) | dynamic-update-slice | bytes 262148 | tf_op jit(solution)/shard_map/while/body/jit(dynamic_update_index_in_dim)/dynamic_update_slice | solution.py:94
  190.6 6.6 %dynamic_update_slice.29 = bf16[16,256,256]{2,0,1:T(8,128)(2,1)} dynamic-update-slice(bf16[16,256,256]{2,0,1:T(8,128)(2,1)} %get-tuple-element.385, bf16[1,256,256]{2,0,1:T(2,128)(2,1)S(1)} %copy.82, s32[]{:T(128)} %get-tuple-element.384, s32[]{:T(128)} %constant.40.clone.1..sunk, s32[]{:T(128)} %constant.40.clone.1..sunk) | dynamic-update-slice | bytes 262148 | tf_op jit(solution)/shard_map/while/body/jit(dynamic_update_index_in_dim)/dynamic_update_slice | solution.py:94
  202.6 6.6 %dynamic_update_slice.29 = bf16[16,256,256]{2,0,1:T(8,128)(2,1)} dynamic-update-slice(bf16[16,256,256]{2,0,1:T(8,128)(2,1)} %get-tuple-element.385, bf16[1,256,256]{2,0,1:T(2,128)(2,1)S(1)} %copy.82, s32[]{:T(128)} %get-tuple-element.384, s32[]{:T(128)} %constant.40.clone.1..sunk, s32[]{:T(128)} %constant.40.clone.1..sunk) | dynamic-update-slice | bytes 262148 | tf_op jit(solution)/shard_map/while/body/jit(dynamic_update_index_in_dim)/dynamic_update_slice | solution.py:94
  214.6 6.6 %dynamic_update_slice.29 = bf16[16,256,256]{2,0,1:T(8,128)(2,1)} dynamic-update-slice(bf16[16,256,256]{2,0,1:T(8,128)(2,1)} %get-tuple-element.385, bf16[1,256,256]{2,0,1:T(2,128)(2,1)S(1)} %copy.82, s32[]{:T(128)} %get-tuple-element.384, s32[]{:T(128)} %constant.40.clone.1..sunk, s32[]{:T(128)} %constant.40.clone.1..sunk) | dynamic-update-slice | bytes 262148 | tf_op jit(solution)/shard_map/while/body/jit(dynamic_update_index_in_dim)/dynamic_update_slice | solution.py:94
  226.5 6.6 %dynamic_update_slice.29 = bf16[16,256,256]{2,0,1:T(8,128)(2,1)} dynamic-update-slice(bf16[16,256,256]{2,0,1:T(8,128)(2,1)} %get-tuple-element.385, bf16[1,256,256]{2,0,1:T(2,128)(2,1)S(1)} %copy.82, s32[]{:T(128)} %get-tuple-element.384, s32[]{:T(128)} %constant.40.clone.1..sunk, s32[]{:T(128)} %constant.40.clone.1..sunk) | dynamic-update-slice | bytes 262148 | tf_op jit(solution)/shard_map/while/body/jit(dynamic_update_index_in_dim)/dynamic_update_slice | solution.py:94
  238.5 6.6 %dynamic_update_slice.29 = bf16[16,256,256]{2,0,1:T(8,128)(2,1)} dynamic-update-slice(bf16[16,256,256]{2,0,1:T(8,128)(2,1)} %get-tuple-element.385, bf16[1,256,256]{2,0,1:T(2,128)(2,1)S(1)} %copy.82, s32[]{:T(128)} %get-tuple-element.384, s32[]{:T(128)} %constant.40.clone.1..sunk, s32[]{:T(128)} %constant.40.clone.1..sunk) | dynamic-update-slice | bytes 262148 | tf_op jit(solution)/shard_map/while/body/jit(dynamic_update_index_in_dim)/dynamic_update_slice | solution.py:94
  250.5 6.6 %dynamic_update_slice.29 = bf16[16,256,256]{2,0,1:T(8,128)(2,1)} dynamic-update-slice(bf16[16,256,256]{2,0,1:T(8,128)(2,1)} %get-tuple-element.385, bf16[1,256,256]{2,0,1:T(2,128)(2,1)S(1)} %copy.82, s32[]{:T(128)} %get-tuple-element.384, s32[]{:T(128)} %constant.40.clone.1..sunk, s32[]{:T(128)} %constant.40.clone.1..sunk) | dynamic-update-slice | bytes 262148 | tf_op jit(solution)/shard_map/while/body/jit(dynamic_update_index_in_dim)/dynamic_update_slice | solution.py:94
  262.4 6.6 %dynamic_update_slice.29 = bf16[16,256,256]{2,0,1:T(8,128)(2,1)} dynamic-update-slice(bf16[16,256,256]{2,0,1:T(8,128)(2,1)} %get-tuple-element.385, bf16[1,256,256]{2,0,1:T(2,128)(2,1)S(1)} %copy.82, s32[]{:T(128)} %get-tuple-element.384, s32[]{:T(128)} %constant.40.clone.1..sunk, s32[]{:T(128)} %constant.40.clone.1..sunk) | dynamic-update-slice | bytes 262148 | tf_op jit(solution)/shard_map/while/body/jit(dynamic_update_index_in_dim)/dynamic_update_slice | solution.py:94
  274.4 6.6 %dynamic_update_slice.29 = bf16[16,256,256]{2,0,1:T(8,128)(2,1)} dynamic-update-slice(bf16[16,256,256]{2,0,1:T(8,128)(2,1)} %get-tuple-element.385, bf16[1,256,256]{2,0,1:T(2,128)(2,1)S(1)} %copy.82, s32[]{:T(128)} %get-tuple-element.384, s32[]{:T(128)} %constant.40.clone.1..sunk, s32[]{:T(128)} %constant.40.clone.1..sunk) | dynamic-update-slice | bytes 262148 | tf_op jit(solution)/shard_map/while/body/jit(dynamic_update_index_in_dim)/dynamic_update_slice | solution.py:94
  281.3 1.1 reshape.134
  282.4 6.5 %all-to-all-start.1 = ((f32[16,1,1024]{2,1,0:T(1,128)}), f32[16,1,1024]{2,1,0:T(1,128)S(1)}, u32[]{:S(2)}, u32[]{:S(2)}) async-start(f32[16,1,1024]{2,1,0:T(1,128)} %reshape.134), calls=%async_computation.1 | async-start | bytes 131072 | tf_op jit(solution)/shard_map/all_to_all | solution.py:101
  289.6 3.6 all-to-all-done.1
  293.2 9.5 %all_to_all.45 = f32[16,1,1024]{2,1,0:T(1,128)S(1)} all-to-all(f32[16,1,1024]{2,1,0:T(1,128)S(1)} %reshape.136), channel_id=1, replica_groups=mesh['groups'=2,'seq'=16] {'seq'}, dimensions={0} | all-to-all | bytes 131072 | tf_op jit(solution)/shard_map/all_to_all | solution.py:102
  302.6 7.1 %all-to-all-start = ((bf16[1,16,256,256]{3,1,0,2:T(8,128)(2,1)}), bf16[1,16,256,256]{3,1,0,2:T(8,128)(2,1)}, u32[]{:S(2)}, u32[]{:S(2)}) async-start(bf16[1,16,256,256]{3,1,0,2:T(8,128)(2,1)} %bitcast.75), calls=%async_computation | async-start | bytes 4194304 | tf_op jit(solution)/shard_map/all_to_all | solution.py:97
  314.5 1.6 copy.56
  316.1 7.0 %mul.52 = f32[16,16,16,4,64]{4,3,2,0,1:T(4,128)} broadcast(f32[16,16,16,4]{3,2,0,1:T(8,128)S(1)} %copy.56), dimensions={0,1,2,3} | broadcast | bytes 4259840 | tf_op jit(solution)/shard_map/mul | solution.py:109
  323.1 8.6 %mul.53 = f32[16,1,16,16,256]{4,3,0,2,1:T(8,128)} reshape(f32[16,16,16,4,64]{4,3,2,0,1:T(4,128)} %mul.52) | data formatting | bytes 8388608 | tf_op jit(solution)/shard_map/mul | solution.py:109
  332.6 24.7 %all-to-all-done = bf16[1,16,256,256]{3,1,0,2:T(8,128)(2,1)} async-done(((bf16[1,16,256,256]{3,1,0,2:T(8,128)(2,1)}), bf16[1,16,256,256]{3,1,0,2:T(8,128)(2,1)}, u32[]{:S(2)}, u32[]{:S(2)}) %all-to-all-start) | async-done | bytes 2097184 | tf_op jit(solution)/shard_map/all_to_all | solution.py:97
  357.2 2.4 copy.53
  361.3 1.2 fusion.19
  (463 shorter events, 170.6 us)
Async XLA Ops:
  7.2 354.1 %copy-start = (bf16[256,512]{1,0:T(8,128)(2,1)S(1)}, bf16[256,512]{1,0:T(8,128)(2,1)}, u32[]{:S(2)}) copy-start(bf16[256,512]{1,0:T(8,128)(2,1)} %param.27) | copy-start | bytes 786436
  7.2 82.3 %all-gather.2.cloned.1.call-start = ((), (), s32[]{:S(2)}) async-start(), calls=%async_computation.3 | async-start | bytes 2228224 | tf_op jit(solution)/shard_map/all_gather | solution.py:72
  9.1 80.3 %copy-start.7 = (s32[16]{0:T(128)S(1)}, s32[16]{0:T(128)}, u32[]{:S(2)}) copy-start(s32[16]{0:T(128)} %param.20) | copy-start | bytes 196
  9.2 3.0 copy-start.3
  9.2 4.0 %copy-start.2 = (bf16[256,256]{1,0:T(8,128)(2,1)S(1)}, bf16[256,256]{1,0:T(8,128)(2,1)}, u32[]{:S(2)}) copy-start(bf16[256,256]{1,0:T(8,128)(2,1)} %get-tuple-element.371) | copy-start | bytes 393220 | tf_op jit(solution)/shard_map/while
  14.2 3.0 copy-start.3
  14.2 4.0 %copy-start.2 = (bf16[256,256]{1,0:T(8,128)(2,1)S(1)}, bf16[256,256]{1,0:T(8,128)(2,1)}, u32[]{:S(2)}) copy-start(bf16[256,256]{1,0:T(8,128)(2,1)} %get-tuple-element.371) | copy-start | bytes 393220 | tf_op jit(solution)/shard_map/while
  19.1 3.0 copy-start.3
  19.1 4.0 %copy-start.2 = (bf16[256,256]{1,0:T(8,128)(2,1)S(1)}, bf16[256,256]{1,0:T(8,128)(2,1)}, u32[]{:S(2)}) copy-start(bf16[256,256]{1,0:T(8,128)(2,1)} %get-tuple-element.371) | copy-start | bytes 393220 | tf_op jit(solution)/shard_map/while
  24.2 3.0 copy-start.3
  24.2 4.0 %copy-start.2 = (bf16[256,256]{1,0:T(8,128)(2,1)S(1)}, bf16[256,256]{1,0:T(8,128)(2,1)}, u32[]{:S(2)}) copy-start(bf16[256,256]{1,0:T(8,128)(2,1)} %get-tuple-element.371) | copy-start | bytes 393220 | tf_op jit(solution)/shard_map/while
  29.2 3.0 copy-start.3
  29.2 4.0 %copy-start.2 = (bf16[256,256]{1,0:T(8,128)(2,1)S(1)}, bf16[256,256]{1,0:T(8,128)(2,1)}, u32[]{:S(2)}) copy-start(bf16[256,256]{1,0:T(8,128)(2,1)} %get-tuple-element.371) | copy-start | bytes 393220 | tf_op jit(solution)/shard_map/while
  34.2 3.0 copy-start.3
  34.2 4.0 %copy-start.2 = (bf16[256,256]{1,0:T(8,128)(2,1)S(1)}, bf16[256,256]{1,0:T(8,128)(2,1)}, u32[]{:S(2)}) copy-start(bf16[256,256]{1,0:T(8,128)(2,1)} %get-tuple-element.371) | copy-start | bytes 393220 | tf_op jit(solution)/shard_map/while
  39.2 3.0 copy-start.3
  39.2 4.0 %copy-start.2 = (bf16[256,256]{1,0:T(8,128)(2,1)S(1)}, bf16[256,256]{1,0:T(8,128)(2,1)}, u32[]{:S(2)}) copy-start(bf16[256,256]{1,0:T(8,128)(2,1)} %get-tuple-element.371) | copy-start | bytes 393220 | tf_op jit(solution)/shard_map/while
  44.2 3.0 copy-start.3
  44.3 4.0 %copy-start.2 = (bf16[256,256]{1,0:T(8,128)(2,1)S(1)}, bf16[256,256]{1,0:T(8,128)(2,1)}, u32[]{:S(2)}) copy-start(bf16[256,256]{1,0:T(8,128)(2,1)} %get-tuple-element.371) | copy-start | bytes 393220 | tf_op jit(solution)/shard_map/while
  49.3 3.1 copy-start.3
  49.3 4.1 %copy-start.2 = (bf16[256,256]{1,0:T(8,128)(2,1)S(1)}, bf16[256,256]{1,0:T(8,128)(2,1)}, u32[]{:S(2)}) copy-start(bf16[256,256]{1,0:T(8,128)(2,1)} %get-tuple-element.371) | copy-start | bytes 393220 | tf_op jit(solution)/shard_map/while
  54.3 4.0 %copy-start.2 = (bf16[256,256]{1,0:T(8,128)(2,1)S(1)}, bf16[256,256]{1,0:T(8,128)(2,1)}, u32[]{:S(2)}) copy-start(bf16[256,256]{1,0:T(8,128)(2,1)} %get-tuple-element.371) | copy-start | bytes 393220 | tf_op jit(solution)/shard_map/while
  59.3 4.0 %copy-start.2 = (bf16[256,256]{1,0:T(8,128)(2,1)S(1)}, bf16[256,256]{1,0:T(8,128)(2,1)}, u32[]{:S(2)}) copy-start(bf16[256,256]{1,0:T(8,128)(2,1)} %get-tuple-element.371) | copy-start | bytes 393220 | tf_op jit(solution)/shard_map/while
  64.4 4.0 %copy-start.2 = (bf16[256,256]{1,0:T(8,128)(2,1)S(1)}, bf16[256,256]{1,0:T(8,128)(2,1)}, u32[]{:S(2)}) copy-start(bf16[256,256]{1,0:T(8,128)(2,1)} %get-tuple-element.371) | copy-start | bytes 393220 | tf_op jit(solution)/shard_map/while
  69.4 4.0 %copy-start.2 = (bf16[256,256]{1,0:T(8,128)(2,1)S(1)}, bf16[256,256]{1,0:T(8,128)(2,1)}, u32[]{:S(2)}) copy-start(bf16[256,256]{1,0:T(8,128)(2,1)} %get-tuple-element.371) | copy-start | bytes 393220 | tf_op jit(solution)/shard_map/while
  74.4 4.0 %copy-start.2 = (bf16[256,256]{1,0:T(8,128)(2,1)S(1)}, bf16[256,256]{1,0:T(8,128)(2,1)}, u32[]{:S(2)}) copy-start(bf16[256,256]{1,0:T(8,128)(2,1)} %get-tuple-element.371) | copy-start | bytes 393220 | tf_op jit(solution)/shard_map/while
  79.4 4.0 %copy-start.2 = (bf16[256,256]{1,0:T(8,128)(2,1)S(1)}, bf16[256,256]{1,0:T(8,128)(2,1)}, u32[]{:S(2)}) copy-start(bf16[256,256]{1,0:T(8,128)(2,1)} %get-tuple-element.371) | copy-start | bytes 393220 | tf_op jit(solution)/shard_map/while
  84.4 4.0 %copy-start.2 = (bf16[256,256]{1,0:T(8,128)(2,1)S(1)}, bf16[256,256]{1,0:T(8,128)(2,1)}, u32[]{:S(2)}) copy-start(bf16[256,256]{1,0:T(8,128)(2,1)} %get-tuple-element.371) | copy-start | bytes 393220 | tf_op jit(solution)/shard_map/while
  282.4 10.8 %all-to-all-start.1 = ((f32[16,1,1024]{2,1,0:T(1,128)}), f32[16,1,1024]{2,1,0:T(1,128)S(1)}, u32[]{:S(2)}, u32[]{:S(2)}) async-start(f32[16,1,1024]{2,1,0:T(1,128)} %reshape.134), calls=%async_computation.1 | async-start | bytes 131072 | tf_op jit(solution)/shard_map/all_to_all | solution.py:101
  302.6 7.1 %copy-start.6 = (bf16[512]{0:T(512)(128)(2,1)S(1)}, bf16[512]{0:T(512)(128)(2,1)}, u32[]{:S(2)}) copy-start(bf16[512]{0:T(512)(128)(2,1)} %param.29) | copy-start | bytes 3076
  302.6 54.6 %all-to-all-start = ((bf16[1,16,256,256]{3,1,0,2:T(8,128)(2,1)}), bf16[1,16,256,256]{3,1,0,2:T(8,128)(2,1)}, u32[]{:S(2)}, u32[]{:S(2)}) async-start(bf16[1,16,256,256]{3,1,0,2:T(8,128)(2,1)} %bitcast.75), calls=%async_computation | async-start | bytes 4194304 | tf_op jit(solution)/shard_map/all_to_all | solution.py:97
  323.1 8.6 %copy-start.4 = (f32[16,4,16]{2,1,0:T(4,128)S(1)}, f32[16,4,16]{2,1,0:T(4,128)}, u32[]{:S(2)}) copy-start(f32[16,4,16]{2,1,0:T(4,128)} %get-tuple-element.229) | copy-start | bytes 12292
  (28 other events, 73.3 us)
Sparse Core Ops, SparseCore 0:
  10.7 42.2 all-gather.1
where the time goes:
time: 374 us; the launch traced here: 369 us
  local copies, waits for them, and re-layouts  217 us (58%)
  matrix products  54.2 us (14%)
  other arithmetic  31.3 us (8%)
  waiting for transfers between devices  28.2 us (8%)
  between operations  14.2 us (4%)
  starting transfers between devices  13.6 us (4%)
  blocking collectives  9.45 us (3%)
    dynamic_update_slice x48, local copies, waits for them, and re-layouts, on_device(): lax.map(local_partials, (queries, all_keys, all_values, live_mask))  109 us
    dynamic_slice x112, local copies, waits for them, and re-layouts, on_device(): lax.map(local_partials, (queries, all_keys, all_values, live_mask))  52.3 us
    dynamic_slice x32, local copies, waits for them, and re-layouts, on_device(): all_keys, all_values = lax.map(project, (codes, scale_index))  27 us
    all_to_all x1, waiting for transfers between devices, on_device(): lax.all_to_all(numerators[None].astype(jnp.bfloat16), 'seq', split_axis=2...  24.7 us
    dot_general x16, matrix products, project(): jnp.dot(history, value_weight, preferred_element_type=jnp.float32)  15.9 us
    dot_general x16, matrix products, project(): jnp.dot(history, key_weight, preferred_element_type=jnp.float32)  15.8 us
    mul x2, local copies, waits for them, and re-layouts, on_device(): got_numerators.reshape(sources, user_count, cand_local, HEADS, head_size)  15.6 us
    reduce_sum x16, other arithmetic, local_partials(): jnp.sum(weights, axis=2)  10.1 us
  transfers between devices with their start and end apart: 3, of which 2 were waited for; matrix products, arithmetic and copies ran while one was open for 28% of the time, Pallas kernels for 0%

commit v1 on v0

--- a/solution.py
+++ b/solution.py
@@ -6,6 +6,13 @@
 
 HEADS = 4
 NEG_FILL = -1e30
+
+
+def trade_parts(x, mesh_axis, split, join):
+    devices = lax.axis_size(mesh_axis)
+    pieces = jnp.stack(jnp.split(x, devices, axis=split), axis=0)
+    pieces = lax.all_to_all(pieces, mesh_axis, split_axis=0, concat_axis=0)
+    return jnp.concatenate(pieces, axis=join)
 
 
 def unpack_codes(words):
@@ -94,9 +101,9 @@
     numerators, totals, peak_rows = lax.map(
         local_partials, (queries, all_keys, all_values, live_mask)
     )
-    got_numerators = lax.all_to_all(
-        numerators[None].astype(jnp.bfloat16), "seq", split_axis=2, concat_axis=0, tiled=True
-    ).astype(jnp.float32)
+    got_numerators = trade_parts(numerators[None].astype(jnp.bfloat16), "seq", 2, 0).astype(
+        jnp.float32
+    )
     got_peaks, got_totals = (
         lax.all_to_all(peak_rows[None], "seq", split_axis=3, concat_axis=0, tiled=True),
         lax.all_to_all(totals[None], "seq", split_axis=3, concat_axis=0, tiled=True),

time: 374 us -> 295 us (0.79)
  local copies, waits for them, and re-layouts: 217 us -> 136 us
  blocking collectives: 9.45 us -> 0 us
  starting transfers between devices: 13.6 us -> 19.5 us
  waiting for transfers between devices: 28.2 us -> 32.1 us
    dynamic_update_slice x48, local copies, waits for them, and re-layouts: 109 us -> 12.4 us  [on_device(): lax.map(local_partials, (queries, all_keys, all_values, live_mask))]
    unnamed x25 -> x39, local copies, waits for them, and re-layouts: 2.97 us -> 21.5 us
    all_to_all x1 -> x0, blocking collectives: 9.45 us -> none  [on_device(): lax.all_to_all(totals[None], 'seq', split_axis=3, concat_axis=0, tiled=True)]
    all_to_all x1 -> x2, starting transfers between devices: 7.07 us -> 13 us  [the longest x1 6.94 us: trade_parts(): pieces = lax.all_to_all(pieces, mesh_axis, split_axis=0, concat_axis=0)]
    all_to_all x1 -> x2, waiting for transfers between devices: 24.7 us -> 29.8 us  [the longest x1 26.1 us: trade_parts(): pieces = lax.all_to_all(pieces, mesh_axis, split_axis=0, concat_axis=0)]
  transfers between devices with their start and end apart: 3 -> 4, of which waited for: 2 -> 3; matrix products, arithmetic and copies ran while one was open for 28% -> 36% of each run, Pallas kernels for 0% -> 0%
where the time goes in v1:
time: 295 us; the launch traced here: 292 us
  local copies, waits for them, and re-layouts  136 us (46%)
  matrix products  54.4 us (18%)
  other arithmetic  33.8 us (11%)
  waiting for transfers between devices  32.1 us (11%)
  starting transfers between devices  19.5 us (7%)
  between operations  14.3 us (5%)
    dynamic_slice x112, local copies, waits for them, and re-layouts, on_device(): lax.map(local_partials, (queries, all_keys, all_values, live_mask))  52.3 us
    dynamic_slice x32, local copies, waits for them, and re-layouts, on_device(): all_keys, all_values = lax.map(project, (codes, scale_index))  27 us
    all_to_all x1, waiting for transfers between devices, trade_parts(): pieces = lax.all_to_all(pieces, mesh_axis, split_axis=0, concat_axis=0)  26.1 us
    unnamed x39, local copies, waits for them, and re-layouts  21.5 us
    dot_general x16, matrix products, project(): jnp.dot(history, value_weight, preferred_element_type=jnp.float32)  15.9 us
    dot_general x16, matrix products, project(): jnp.dot(history, key_weight, preferred_element_type=jnp.float32)  15.8 us
    mul x2, local copies, waits for them, and re-layouts, on_device(): got_numerators.reshape(sources, user_count, cand_local, HEADS, head_size)  15.6 us
    dynamic_update_slice x48, local copies, waits for them, and re-layouts, on_device(): lax.map(local_partials, (queries, all_keys, all_values, live_mask))  12.4 us
  transfers between devices with their start and end apart: 4, of which 3 were waited for; matrix products, arithmetic and copies ran while one was open for 36% of the time, Pallas kernels for 0%

profile of v1, /device:TPU:13, one launch (start us, length us, event | category | flops | bytes accessed | tf_op | source)
XLA Modules:
  0.0 291.5 jit_solution(3946409490598535527)
XLA Ops:
  7.2 1.8 convolution_convert_fusion.3
  9.1 80.3 %while.28 = (s32[]{:T(128)}, bf16[16,512,256]{2,1,0:T(8,128)(2,1)}, bf16[16,512,256]{2,1,0:T(8,128)(2,1)}, s32[16,128,256]{2,1,0:T(8,128)}, s32[16,512]{1,0:T(8,...) while((s32[]{:T(128)}, bf16[16,512,256]{2,1,0:T(8,128)(2,1)}, ...), condition=%wide.region_2.3_spmd.clone, body=%wide.region_0.2_spmd.clone.sunk | while | flops 136183296 | bytes 5916857 | solution.py:100
  27.2 1.0 fusion.81
  37.2 1.0 fusion.81
  49.3 1.0 constant_dynamic-slice_fusion.13
  53.3 1.0 fusion.80
  62.4 1.0 fusion.81
  67.4 1.0 fusion.81
  73.4 1.0 fusion.80
  87.4 1.0 fusion.81
  89.5 94.8 %while.27 = (s32[]{:T(128)}, bf16[16,256,256]{2,1,0:T(8,128)(2,1)}, f32[16,4,256]{2,1,0:T(4,128)S(1)}, f32[16,4,256]{2,1,0:T(4,128)S(1)}, bf16[16,512,256]{2,1,0...) while((s32[]{:T(128)}, bf16[16,256,256]{2,1,0:T(8,128)(2,1)}, ...), condition=%wide.region_6.7_spmd, body=%wide.region_3.6_spmd.sunk | while | flops 141031424 | bytes 10259569 | solution.py:101
  184.3 1.7 fusion.44
  186.0 1.6 fusion.43
  187.5 1.6 fusion.42
  189.1 1.6 fusion.41
  190.7 1.6 fusion.40
  192.2 1.6 fusion.39
  193.8 1.6 fusion.38
  195.4 1.6 fusion.37
  201.2 1.0 reshape.132
  202.2 6.5 %all-to-all-start.1 = ((f32[16,1,1024]{2,1,0:T(1,128)}), f32[16,1,1024]{2,1,0:T(1,128)S(1)}, u32[]{:S(2)}, u32[]{:S(2)}) async-start(f32[16,1,1024]{2,1,0:T(1,128)} %reshape.132), calls=%async_computation.1 | async-start | bytes 131072 | tf_op jit(solution)/shard_map/all_to_all | solution.py:108
  209.0 1.1 reshape.134
  210.7 2.3 all-to-all-done.1
  213.0 6.0 %all-to-all-start.2 = ((f32[16,1,1024]{2,1,0:T(1,128)}), f32[16,1,1024]{2,1,0:T(1,128)S(1)}, u32[]{:S(2)}, u32[]{:S(2)}) async-start(f32[16,1,1024]{2,1,0:T(1,128)} %reshape.134), calls=%async_computation.2 | async-start | bytes 131072 | tf_op jit(solution)/shard_map/all_to_all | solution.py:109
  219.7 3.6 %all-to-all-done.2 = f32[16,1,1024]{2,1,0:T(1,128)S(1)} async-done(((f32[16,1,1024]{2,1,0:T(1,128)}), f32[16,1,1024]{2,1,0:T(1,128)S(1)}, u32[]{:S(2)}, u32[]{:S(2)}) %all-to-all-start.2) | async-done | bytes 65568 | tf_op jit(solution)/shard_map/all_to_all | solution.py:109
  223.3 6.9 %all-to-all-start = ((bf16[16,1,16,16,256]{4,3,2,1,0:T(8,128)(2,1)}), bf16[16,1,16,16,256]{4,3,2,1,0:T(8,128)(2,1)}, u32[]{:S(2)}, u32[]{:S(2)}) async-start(bf16[16,1,16,16,256]{4,3,2,1,0:T(8,128)(2,1)} %fusion.29), calls=%async_computation | async-start | bytes 4194304 | tf_op jit(solution)/shard_map/all_to_all | solution.py:14
  234.5 1.6 copy.55
  236.1 7.0 %mul.52 = f32[16,16,16,4,64]{4,3,2,1,0:T(4,128)} broadcast(f32[16,16,16,4]{3,2,1,0:T(8,128)S(1)} %copy.55), dimensions={0,1,2,3} | broadcast | bytes 4259840 | tf_op jit(solution)/shard_map/mul | solution.py:116
  243.1 8.6 %mul.53 = f32[16,1,16,16,256]{4,3,2,1,0:T(8,128)} reshape(f32[16,16,16,4,64]{4,3,2,1,0:T(4,128)} %mul.52) | data formatting | bytes 8388608 | tf_op jit(solution)/shard_map/mul | solution.py:116
  251.7 26.1 %all-to-all-done = bf16[16,1,16,16,256]{4,3,2,1,0:T(8,128)(2,1)} async-done(((bf16[16,1,16,16,256]{4,3,2,1,0:T(8,128)(2,1)}), bf16[16,1,16,16,256]{4,3,2,1,0:T(8,128)(2,1)}, u32[]{:S(2)}, u32[]{:S(2)}) %all-to-all-start) | async-done | bytes 2097184 | tf_op jit(solution)/shard_map/all_to_all | solution.py:14
  277.8 3.6 %multiply_reduce_fusion = f32[16,16,256]{2,1,0:T(8,128)S(1)} fusion(f32[16,1,16,16,256]{4,3,2,1,0:T(8,128)} %mul.53, bf16[16,1,16,16,256]{4,3,2,1,0:T(8,128)(2,1)} %all-to-all-done), kind=kLoop, calls=%fused_computation.34 | loop fusion | flops 3080192 | bytes 6553600 | tf_op jit(solution)/shard_map/reduce_sum | solution.py:119
  283.4 1.2 fusion.18
  (476 shorter events, 177.8 us)
Async XLA Ops:
  7.2 276.3 %copy-start = (bf16[256,512]{1,0:T(8,128)(2,1)S(1)}, bf16[256,512]{1,0:T(8,128)(2,1)}, u32[]{:S(2)}) copy-start(bf16[256,512]{1,0:T(8,128)(2,1)} %param.27) | copy-start | bytes 786436
  7.2 82.3 %all-gather.2.cloned.1.call-start = ((), (), s32[]{:S(2)}) async-start(), calls=%async_computation.3 | async-start | bytes 2228224 | tf_op jit(solution)/shard_map/all_gather | solution.py:79
  9.1 80.3 %copy-start.8 = (s32[16]{0:T(128)S(1)}, s32[16]{0:T(128)}, u32[]{:S(2)}) copy-start(s32[16]{0:T(128)} %param.20) | copy-start | bytes 196
  9.2 3.0 %copy-start.2 = (bf16[256,256]{1,0:T(8,128)(2,1)S(1)}, bf16[256,256]{1,0:T(8,128)(2,1)}, u32[]{:S(2)}) copy-start(bf16[256,256]{1,0:T(8,128)(2,1)} %get-tuple-element.372) | copy-start | bytes 393220 | tf_op jit(solution)/shard_map/while
  9.2 4.0 %copy-start.1 = (bf16[256,256]{1,0:T(8,128)(2,1)S(1)}, bf16[256,256]{1,0:T(8,128)(2,1)}, u32[]{:S(2)}) copy-start(bf16[256,256]{1,0:T(8,128)(2,1)} %get-tuple-element.371) | copy-start | bytes 393220 | tf_op jit(solution)/shard_map/while
  14.2 3.0 %copy-start.2 = (bf16[256,256]{1,0:T(8,128)(2,1)S(1)}, bf16[256,256]{1,0:T(8,128)(2,1)}, u32[]{:S(2)}) copy-start(bf16[256,256]{1,0:T(8,128)(2,1)} %get-tuple-element.372) | copy-start | bytes 393220 | tf_op jit(solution)/shard_map/while
  14.2 4.0 %copy-start.1 = (bf16[256,256]{1,0:T(8,128)(2,1)S(1)}, bf16[256,256]{1,0:T(8,128)(2,1)}, u32[]{:S(2)}) copy-start(bf16[256,256]{1,0:T(8,128)(2,1)} %get-tuple-element.371) | copy-start | bytes 393220 | tf_op jit(solution)/shard_map/while
  19.1 3.0 %copy-start.2 = (bf16[256,256]{1,0:T(8,128)(2,1)S(1)}, bf16[256,256]{1,0:T(8,128)(2,1)}, u32[]{:S(2)}) copy-start(bf16[256,256]{1,0:T(8,128)(2,1)} %get-tuple-element.372) | copy-start | bytes 393220 | tf_op jit(solution)/shard_map/while
  19.1 4.0 %copy-start.1 = (bf16[256,256]{1,0:T(8,128)(2,1)S(1)}, bf16[256,256]{1,0:T(8,128)(2,1)}, u32[]{:S(2)}) copy-start(bf16[256,256]{1,0:T(8,128)(2,1)} %get-tuple-element.371) | copy-start | bytes 393220 | tf_op jit(solution)/shard_map/while
  24.2 3.0 %copy-start.2 = (bf16[256,256]{1,0:T(8,128)(2,1)S(1)}, bf16[256,256]{1,0:T(8,128)(2,1)}, u32[]{:S(2)}) copy-start(bf16[256,256]{1,0:T(8,128)(2,1)} %get-tuple-element.372) | copy-start | bytes 393220 | tf_op jit(solution)/shard_map/while
  24.2 4.0 %copy-start.1 = (bf16[256,256]{1,0:T(8,128)(2,1)S(1)}, bf16[256,256]{1,0:T(8,128)(2,1)}, u32[]{:S(2)}) copy-start(bf16[256,256]{1,0:T(8,128)(2,1)} %get-tuple-element.371) | copy-start | bytes 393220 | tf_op jit(solution)/shard_map/while
  29.2 3.0 %copy-start.2 = (bf16[256,256]{1,0:T(8,128)(2,1)S(1)}, bf16[256,256]{1,0:T(8,128)(2,1)}, u32[]{:S(2)}) copy-start(bf16[256,256]{1,0:T(8,128)(2,1)} %get-tuple-element.372) | copy-start | bytes 393220 | tf_op jit(solution)/shard_map/while
  29.2 4.0 %copy-start.1 = (bf16[256,256]{1,0:T(8,128)(2,1)S(1)}, bf16[256,256]{1,0:T(8,128)(2,1)}, u32[]{:S(2)}) copy-start(bf16[256,256]{1,0:T(8,128)(2,1)} %get-tuple-element.371) | copy-start | bytes 393220 | tf_op jit(solution)/shard_map/while
  34.2 3.0 %copy-start.2 = (bf16[256,256]{1,0:T(8,128)(2,1)S(1)}, bf16[256,256]{1,0:T(8,128)(2,1)}, u32[]{:S(2)}) copy-start(bf16[256,256]{1,0:T(8,128)(2,1)} %get-tuple-element.372) | copy-start | bytes 393220 | tf_op jit(solution)/shard_map/while
  34.2 4.0 %copy-start.1 = (bf16[256,256]{1,0:T(8,128)(2,1)S(1)}, bf16[256,256]{1,0:T(8,128)(2,1)}, u32[]{:S(2)}) copy-start(bf16[256,256]{1,0:T(8,128)(2,1)} %get-tuple-element.371) | copy-start | bytes 393220 | tf_op jit(solution)/shard_map/while
  39.2 4.0 %copy-start.1 = (bf16[256,256]{1,0:T(8,128)(2,1)S(1)}, bf16[256,256]{1,0:T(8,128)(2,1)}, u32[]{:S(2)}) copy-start(bf16[256,256]{1,0:T(8,128)(2,1)} %get-tuple-element.371) | copy-start | bytes 393220 | tf_op jit(solution)/shard_map/while
  44.2 3.0 %copy-start.2 = (bf16[256,256]{1,0:T(8,128)(2,1)S(1)}, bf16[256,256]{1,0:T(8,128)(2,1)}, u32[]{:S(2)}) copy-start(bf16[256,256]{1,0:T(8,128)(2,1)} %get-tuple-element.372) | copy-start | bytes 393220 | tf_op jit(solution)/shard_map/while
  44.3 4.0 %copy-start.1 = (bf16[256,256]{1,0:T(8,128)(2,1)S(1)}, bf16[256,256]{1,0:T(8,128)(2,1)}, u32[]{:S(2)}) copy-start(bf16[256,256]{1,0:T(8,128)(2,1)} %get-tuple-element.371) | copy-start | bytes 393220 | tf_op jit(solution)/shard_map/while
  49.3 3.1 %copy-start.2 = (bf16[256,256]{1,0:T(8,128)(2,1)S(1)}, bf16[256,256]{1,0:T(8,128)(2,1)}, u32[]{:S(2)}) copy-start(bf16[256,256]{1,0:T(8,128)(2,1)} %get-tuple-element.372) | copy-start | bytes 393220 | tf_op jit(solution)/shard_map/while
  49.3 4.1 %copy-start.1 = (bf16[256,256]{1,0:T(8,128)(2,1)S(1)}, bf16[256,256]{1,0:T(8,128)(2,1)}, u32[]{:S(2)}) copy-start(bf16[256,256]{1,0:T(8,128)(2,1)} %get-tuple-element.371) | copy-start | bytes 393220 | tf_op jit(solution)/shard_map/while
  54.3 4.0 %copy-start.1 = (bf16[256,256]{1,0:T(8,128)(2,1)S(1)}, bf16[256,256]{1,0:T(8,128)(2,1)}, u32[]{:S(2)}) copy-start(bf16[256,256]{1,0:T(8,128)(2,1)} %get-tuple-element.371) | copy-start | bytes 393220 | tf_op jit(solution)/shard_map/while
  59.3 4.0 %copy-start.1 = (bf16[256,256]{1,0:T(8,128)(2,1)S(1)}, bf16[256,256]{1,0:T(8,128)(2,1)}, u32[]{:S(2)}) copy-start(bf16[256,256]{1,0:T(8,128)(2,1)} %get-tuple-element.371) | copy-start | bytes 393220 | tf_op jit(solution)/shard_map/while
  64.4 4.0 %copy-start.1 = (bf16[256,256]{1,0:T(8,128)(2,1)S(1)}, bf16[256,256]{1,0:T(8,128)(2,1)}, u32[]{:S(2)}) copy-start(bf16[256,256]{1,0:T(8,128)(2,1)} %get-tuple-element.371) | copy-start | bytes 393220 | tf_op jit(solution)/shard_map/while
  69.4 4.0 %copy-start.1 = (bf16[256,256]{1,0:T(8,128)(2,1)S(1)}, bf16[256,256]{1,0:T(8,128)(2,1)}, u32[]{:S(2)}) copy-start(bf16[256,256]{1,0:T(8,128)(2,1)} %get-tuple-element.371) | copy-start | bytes 393220 | tf_op jit(solution)/shard_map/while
  74.4 4.0 %copy-start.1 = (bf16[256,256]{1,0:T(8,128)(2,1)S(1)}, bf16[256,256]{1,0:T(8,128)(2,1)}, u32[]{:S(2)}) copy-start(bf16[256,256]{1,0:T(8,128)(2,1)} %get-tuple-element.371) | copy-start | bytes 393220 | tf_op jit(solution)/shard_map/while
  79.4 4.0 %copy-start.1 = (bf16[256,256]{1,0:T(8,128)(2,1)S(1)}, bf16[256,256]{1,0:T(8,128)(2,1)}, u32[]{:S(2)}) copy-start(bf16[256,256]{1,0:T(8,128)(2,1)} %get-tuple-element.371) | copy-start | bytes 393220 | tf_op jit(solution)/shard_map/while
  84.4 4.0 %copy-start.1 = (bf16[256,256]{1,0:T(8,128)(2,1)S(1)}, bf16[256,256]{1,0:T(8,128)(2,1)}, u32[]{:S(2)}) copy-start(bf16[256,256]{1,0:T(8,128)(2,1)} %get-tuple-element.371) | copy-start | bytes 393220 | tf_op jit(solution)/shard_map/while
  184.3 12.7 %copy-start.3 = (bf16[16,256,256]{2,1,0:T(8,128)(2,1)S(1)}, bf16[16,256,256]{2,1,0:T(8,128)(2,1)}, u32[]{:S(2)}) copy-start(bf16[16,256,256]{2,1,0:T(8,128)(2,1)} %get-tuple-element.96) | copy-start | bytes 6291460
  202.2 10.8 %all-to-all-start.1 = ((f32[16,1,1024]{2,1,0:T(1,128)}), f32[16,1,1024]{2,1,0:T(1,128)S(1)}, u32[]{:S(2)}, u32[]{:S(2)}) async-start(f32[16,1,1024]{2,1,0:T(1,128)} %reshape.132), calls=%async_computation.1 | async-start | bytes 131072 | tf_op jit(solution)/shard_map/all_to_all | solution.py:108
  213.0 10.4 %all-to-all-start.2 = ((f32[16,1,1024]{2,1,0:T(1,128)}), f32[16,1,1024]{2,1,0:T(1,128)S(1)}, u32[]{:S(2)}, u32[]{:S(2)}) async-start(f32[16,1,1024]{2,1,0:T(1,128)} %reshape.134), calls=%async_computation.2 | async-start | bytes 131072 | tf_op jit(solution)/shard_map/all_to_all | solution.py:109
  219.7 10.6 %copy-start.7 = (bf16[512]{0:T(512)(128)(2,1)S(1)}, bf16[512]{0:T(512)(128)(2,1)}, u32[]{:S(2)}) copy-start(bf16[512]{0:T(512)(128)(2,1)} %param.29) | copy-start | bytes 3076
  223.3 54.5 %all-to-all-start = ((bf16[16,1,16,16,256]{4,3,2,1,0:T(8,128)(2,1)}), bf16[16,1,16,16,256]{4,3,2,1,0:T(8,128)(2,1)}, u32[]{:S(2)}, u32[]{:S(2)}) async-start(bf16[16,1,16,16,256]{4,3,2,1,0:T(8,128)(2,1)} %fusion.29), calls=%async_computation | async-start | bytes 4194304 | tf_op jit(solution)/shard_map/all_to_all | solution.py:14
  (28 other events, 74.0 us)
Sparse Core Ops, SparseCore 0:
  10.7 42.2 all-gather.1
